TPU v7x, 32 devices: a whole 2x2x4 slice. The times are simulated.
32 devices in a mesh: ep: 8 (over y, x, core), dp: 4 (over z).
Axes of the slice: x: 2, y: 2, z: 4, core: 2. Of those that a mesh axis runs over, the one named last changes fastest.
Arguments:
- tokens: bfloat16 [4096, 1792], P(('ep', 'dp')), may hold values from -6 to 6
- cotangent: bfloat16 [4096, 1792], P(('ep', 'dp')), may hold values from -6 to 6
- slot_choice: int32 [4096, 2], P(('ep', 'dp')), may hold values from 0 to 7, all different within a row; in each aligned block of 128 rows (0 to 127, 128 to 255, ...) at most 40 rows name the same one
- gate_values: float32 [4096, 2], P(('ep', 'dp')), may hold values from 0.1 to 1
- slot_expert: int32 [8], replicated, may hold values from 0 to 3, as said below
- gate_weight: bfloat16 [8, 1792, 1280], P('ep', None, 'dp'), as said below
- up_weight: bfloat16 [8, 1792, 1280], P('ep', None, 'dp'), as said below
- down_weight: bfloat16 [8, 1280, 1792], P('ep', 'dp'), as said below
Outputs:
- token_grad: bfloat16 [4096, 1792], P(('ep', 'dp'))
- down_grad: bfloat16 [8, 1280, 1792], P('ep', 'dp')
Inputs may be any that keep to these rules, and one draw needn't show every extreme that they name: `slot_choice`: each row names 2 different slots; among the rows of one device no slot is named more than 40 times, a bound that some block reaches. `slot_expert`: every expert is held by at least one slot. `gate_weight`: slots that hold the same expert have equal matrices. `up_weight`: slots that hold the same expert have equal matrices. `down_weight`: slots that hold the same expert have equal matrices.
All inputs are finite; a program needn't handle non-finite values.
Results may differ from a plain program's by a relative error of at most 0.0098.
Values may be sent and summed in bfloat16 or wider, within the bound.
A program may use at most 128 MiB of HBM per device.

v0:
```python
import jax
import jax.numpy as jnp
from jax import lax
from jax.sharding import PartitionSpec as P


def per_device(
    tokens, cotangent, slot_choice, gate_values, slot_expert, gate_weight, up_weight, down_weight
):
    n_slots = lax.axis_size("ep")
    tok_rows, width = tokens.shape
    topk = slot_choice.shape[1]
    capacity = max(2, 5 * tok_rows * topk // (4 * n_slots))
    rows_out = n_slots * capacity
    flat_slot = slot_choice.reshape(-1)
    onehot = (flat_slot[:, None] == jnp.arange(n_slots, dtype=jnp.int32)[None, :]).astype(jnp.int32)
    position = jnp.sum(jnp.cumsum(onehot, axis=0) * onehot, axis=1) - 1
    dest = flat_slot * capacity + position
    target = (dest[None, :] == jnp.arange(rows_out, dtype=jnp.int32)[:, None]).reshape(
        rows_out, tok_rows, topk
    )
    select = jnp.any(target, axis=2).astype(jnp.bfloat16)
    weight_table = jnp.sum(jnp.where(target, gate_values[None, :, :], 0.0), axis=2)
    sent_x = jnp.dot(select, tokens, preferred_element_type=jnp.float32).astype(jnp.bfloat16)
    sent_g = jnp.dot(
        weight_table,
        cotangent.astype(jnp.float32),
        precision=lax.Precision.HIGHEST,
        preferred_element_type=jnp.float32,
    ).astype(jnp.bfloat16)
    sent_x = sent_x.reshape(n_slots, capacity, width)
    sent_g = sent_g.reshape(n_slots, capacity, width)
    recv_x, recv_g = (
        lax.all_to_all(sent_x, "ep", split_axis=0, concat_axis=0, tiled=True),
        lax.all_to_all(sent_g, "ep", split_axis=0, concat_axis=0, tiled=True),
    )
    all_x, all_g = (
        lax.all_gather(recv_x, "dp", axis=0, tiled=True),
        lax.all_gather(recv_g, "dp", axis=0, tiled=True),
    )
    groups = all_x.shape[0] // n_slots
    rows_x = all_x.reshape(-1, width)
    rows_g = all_g.reshape(-1, width)
    w_gate = gate_weight[0]
    w_up = up_weight[0]
    w_down = down_weight[0]
    gate = jnp.dot(rows_x, w_gate, preferred_element_type=jnp.float32)
    up = jnp.dot(rows_x, w_up, preferred_element_type=jnp.float32)
    sig = jax.nn.sigmoid(gate)
    act = (gate * sig * up).astype(jnp.bfloat16)
    d_act = lax.dot_general(
        rows_g, w_down, (((1,), (1,)), ((), ())), preferred_element_type=jnp.float32
    )
    d_gate = (d_act * up * sig * (1.0 + gate * (1.0 - sig))).astype(jnp.bfloat16)
    d_up = (d_act * gate * sig).astype(jnp.bfloat16)
    partial_value = lax.dot_general(
        d_gate, w_gate, (((1,), (1,)), ((), ())), preferred_element_type=jnp.float32
    )
    partial_value = partial_value + lax.dot_general(
        d_up, w_up, (((1,), (1,)), ((), ())), preferred_element_type=jnp.float32
    )
    partial_value = partial_value.reshape(groups, n_slots, capacity, width)
    summed = lax.psum_scatter(partial_value, "dp", scatter_dimension=0, tiled=True).astype(
        jnp.bfloat16
    )
    back = lax.all_to_all(summed, "ep", split_axis=1, concat_axis=1, tiled=True)
    back = back.reshape(rows_out, width)
    token_grad = lax.dot_general(
        select, back, (((0,), (0,)), ((), ())), preferred_element_type=jnp.float32
    )
    slot_grad = lax.dot_general(
        act, rows_g, (((0,), (0,)), ((), ())), preferred_element_type=jnp.float32
    )
    hidden = slot_grad.shape[0]
    pieces = slot_grad.reshape(n_slots, -1)
    received = lax.all_to_all(pieces, "ep", split_axis=0, concat_axis=0, tiled=True)
    same = (slot_expert[:, None] == slot_expert[None, :]).astype(jnp.float32)
    combined = jnp.dot(
        same, received, precision=lax.Precision.HIGHEST, preferred_element_type=jnp.float32
    )
    returned = lax.all_to_all(
        combined.astype(jnp.bfloat16), "ep", split_axis=0, concat_axis=0, tiled=True
    ).astype(combined.dtype)
    down_grad = returned.reshape(1, hidden, width).astype(jnp.bfloat16)
    return (token_grad.astype(jnp.bfloat16), down_grad)


def solution(mesh):
    return jax.shard_map(
        per_device,
        mesh=mesh,
        in_specs=(
            P(("ep", "dp"), None),
            P(("ep", "dp"), None),
            P(("ep", "dp"), None),
            P(("ep", "dp"), None),
            P(),
            P("ep", None, "dp"),
            P("ep", None, "dp"),
            P("ep", "dp", None),
        ),
        out_specs=(P(("ep", "dp"), None), P("ep", "dp", None)),
        check_vma=False,
    )
```

profile of v0, /device:TPU:0, one launch (start us, length us, event | category | flops | bytes accessed | tf_op | source)
XLA Modules:
  0.0 612.0 jit_solution(7490275403689726438)
XLA Ops:
  7.2 0.9 copy.49
  8.4 0.6 reduce-window.6
  9.5 0.7 multiply_add_fusion
  10.3 1.5 convolution_convert_fusion.1
  11.8 21.6 %all_to_all.40 = bf16[8,40,1792]{2,1,0:T(8,128)(2,1)} all-to-all(bf16[8,40,1792]{2,1,0:T(8,128)(2,1)S(1)} %bitcast.46), channel_id=1, replica_groups=mesh['ep'=8,'dp'=4] {'ep'}, dimensions={0} | all-to-all | bytes 2293760 | tf_op jit(solution)/shard_map/all_to_all | solution.py:34
  33.5 1.0 convolution_convert_fusion.2
  34.6 19.5 %all_to_all.41 = bf16[8,40,1792]{2,1,0:T(8,128)(2,1)} all-to-all(bf16[8,40,1792]{2,1,0:T(8,128)(2,1)S(1)} %bitcast.44), channel_id=1, replica_groups=mesh['ep'=8,'dp'=4] {'ep'}, dimensions={0} | all-to-all | bytes 2293760 | tf_op jit(solution)/shard_map/all_to_all | solution.py:35
  54.2 0.6 dynamic-slice
  54.7 65.4 %all-gather.5.cloned.1.call-done = bf16[32,40,1792]{2,1,0:T(8,128)(2,1)} async-done(((bf16[8,40,1792]{2,1,0:T(8,128)(2,1)}), bf16[32,40,1792]{2,1,0:T(8,128)(2,1)}) %all-gather.5.cloned.1.call-update) | async-done | bytes 4587536 | tf_op jit(solution)/shard_map/all_gather | solution.py:38
  120.2 4.1 fusion.5
  124.3 2.9 fusion.8
  127.2 80.2 %all-gather.3.cloned.1.call-done = bf16[32,40,1792]{2,1,0:T(8,128)(2,1)} async-done(((bf16[8,40,1792]{2,1,0:T(8,128)(2,1)}), bf16[32,40,1792]{2,1,0:T(8,128)(2,1)}) %all-gather.3.cloned.1.call-update) | async-done | bytes 4587536 | tf_op jit(solution)/shard_map/all_gather | solution.py:39
  207.4 5.6 fusion.10
  213.1 3.3 fusion.12
  216.4 6.7 %all_to_all.34 = f32[8,1,71680]{2,1,0:T(1,128)} reshape(f32[320,1792]{1,0:T(8,128)} %fusion.12) | data formatting | bytes 4587520 | tf_op jit(solution)/shard_map/all_to_all | solution.py:76
  223.1 4.5 all-to-all-start.3
  227.7 5.0 fusion.3
  232.7 2.7 convolution_add_fusion
  235.4 4.4 copy.52
  239.9 310.3 %all-reduce.2 = bf16[4,8,40,1792]{3,2,0,1:T(8,128)(2,1)} all-reduce(f32[4,8,40,1792]{3,2,0,1:T(8,128)} %copy.52), channel_id=2, replica_groups=mesh['ep'=8,'dp'=4] {'dp'}, use_global_device_ids=true, to_apply=%region_5.6.clone | all-reduce | flops 2293760 | bytes 13762560
  550.1 3.0 dynamic-slice_convert_fusion
  553.1 3.9 all-to-all-start.2
  557.1 3.4 fusion
  561.0 1.5 reduce.3
  562.5 2.0 reshape.86
  564.4 9.1 %all-to-all-done.2 = bf16[1,8,40,1792]{3,2,0,1:T(8,128)(2,1)S(1)} async-done(((bf16[1,8,40,1792]{3,2,0,1:T(8,128)(2,1)}), bf16[1,8,40,1792]{3,2,0,1:T(8,128)(2,1)S(1)}, u32[]{:S(2)}, u32[]{:S(2)}) %all-to-all-start.2) | async-done | bytes 1146912 | tf_op jit(solution)/shard_map/all_to_all | solution.py:66
  573.5 3.8 all-to-all-start.4
  577.3 1.2 convolution_convert_fusion.3
  578.5 14.9 %all-to-all-done.4 = bf16[8,2,35840]{2,1,0:T(2,128)(2,1)S(1)} async-done(((bf16[8,2,35840]{2,1,0:T(2,128)(2,1)}), bf16[8,2,35840]{2,1,0:T(2,128)(2,1)S(1)}, u32[]{:S(2)}, u32[]{:S(2)}) %all-to-all-start.4) | async-done | bytes 1146912 | tf_op jit(solution)/shard_map/all_to_all | solution.py:81
  593.4 0.9 reshape.87
  594.4 8.0 %reduce.1 = bf16[8,71680]{1,0:T(8,128)(2,1)} reduce(bf16[8,1,71680]{2,1,0:T(2,128)(2,1)S(1)} %reshape.87, bf16[]{:T(256)} %constant.25), dimensions={1}, to_apply=%all_to_all.32.reduce_sub_computation | reduce | bytes 2293762 | tf_op jit(solution)/shard_map/all_to_all | solution.py:81
  602.4 2.8 all_to_all.33
  (42 shorter events, 1.6 us)
Async XLA Ops:
  7.2 113.0 %copy-start = (bf16[1,1792,320]{1,2,0:T(8,128)(2,1)S(1)}, bf16[1,1792,320]{1,2,0:T(8,128)(2,1)}, u32[]{:S(2)}) copy-start(bf16[1,1792,320]{1,2,0:T(8,128)(2,1)} %param.13) | copy-start | bytes 3440644
  7.2 113.0 %all-gather.5.cloned.1.call-start = ((), (), s32[]{:S(2)}) async-start(), calls=%async_computation.6 | async-start | bytes 5734400 | tf_op jit(solution)/shard_map/all_gather | solution.py:38
  11.8 21.7 %copy-start.8 = (f32[128,2]{0,1:T(2,128)S(1)}, f32[128,2]{0,1:T(2,128)}, u32[]{:S(2)}) copy-start(f32[128,2]{0,1:T(2,128)} %param.11) | copy-start | bytes 3076
  11.8 21.8 %copy-start.6 = (bf16[128,1792]{1,0:T(8,128)(2,1)S(1)}, bf16[128,1792]{1,0:T(8,128)(2,1)}, u32[]{:S(2)}) copy-start(bf16[128,1792]{1,0:T(8,128)(2,1)} %param.9) | copy-start | bytes 1376260
  33.4 174.0 %all-gather.3.cloned.1.call-start = ((), (), s32[]{:S(2)}) async-start(), calls=%async_computation.5 | async-start | bytes 5734400 | tf_op jit(solution)/shard_map/all_gather | solution.py:39
  34.6 19.6 %copy-start.11 = (u32[32]{0:T(128)S(1)}, u32[32]{0:T(128)}, u32[]{:S(2)}) copy-start(u32[32]{0:T(128)} %constant.22) | copy-start | bytes 388
  120.2 4.1 copy-start.4
  120.2 4.1 copy-start.9
  207.4 5.6 copy-start.3
  207.4 5.6 copy-start.10
  223.1 330.0 %all-to-all-start.3 = ((f32[8,1,71680]{2,1,0:T(1,128)}), f32[8,1,71680]{2,1,0:T(1,128)}, u32[]{:S(2)}, u32[]{:S(2)}) async-start(f32[8,1,71680]{2,1,0:T(1,128)} %all_to_all.34), calls=%async_computation.3 | async-start | bytes 4587520 | tf_op jit(solution)/shard_map/all_to_all | solution.py:76
  227.7 5.0 copy-start.2
  227.7 5.0 copy-start.5
  553.1 3.9 copy-start.7
  553.1 20.4 %all-to-all-start.2 = ((bf16[1,8,40,1792]{3,2,0,1:T(8,128)(2,1)}), bf16[1,8,40,1792]{3,2,0,1:T(8,128)(2,1)S(1)}, u32[]{:S(2)}, u32[]{:S(2)}) async-start(bf16[1,8,40,1792]{3,2,0,1:T(8,128)(2,1)} %dynamic-slice_convert_fusion), calls=%async_computation.2 | async-start | bytes 2293760 | tf_op jit(solution)/shard_map/all_to_all | solution.py:66
  573.5 19.9 %all-to-all-start.4 = ((bf16[8,2,35840]{2,1,0:T(2,128)(2,1)}), bf16[8,2,35840]{2,1,0:T(2,128)(2,1)S(1)}, u32[]{:S(2)}, u32[]{:S(2)}) async-start(bf16[8,2,35840]{2,1,0:T(2,128)(2,1)} %reshape.86), calls=%async_computation.4 | async-start | bytes 2293760 | tf_op jit(solution)/shard_map/all_to_all | solution.py:81
  594.4 10.8 %copy-start.1 = (bf16[1,1792,320]{1,2,0:T(8,128)(2,1)S(1)}, bf16[1,1792,320]{1,2,0:T(8,128)(2,1)}, u32[]{:S(2)}) copy-start(bf16[1,1792,320]{1,2,0:T(8,128)(2,1)} %param.13) | copy-start | bytes 3440644
Sparse Core Ops, SparseCore 0:
  33.5 86.5 all-gather.4
  121.7 85.6 all-gather.2
where the time goes:
time: 613 us; the launch traced here: 612 us
  blocking collectives  351 us (57%)
  waiting for transfers between devices  170 us (28%)
  matrix products  30.8 us (5%)
  local copies, waits for them, and re-layouts  22.5 us (4%)
  between operations  14.3 us (2%)
  starting transfers between devices  12.3 us (2%)
  other arithmetic  11 us (2%)
    unnamed x1, blocking collectives  310 us
    all_gather x1, waiting for transfers between devices, per_device(): lax.all_gather(recv_g, 'dp', axis=0, tiled=True)  80.2 us
    all_gather x1, waiting for transfers between devices, per_device(): lax.all_gather(recv_x, 'dp', axis=0, tiled=True)  65.4 us
    all_to_all x1, blocking collectives, per_device(): lax.all_to_all(sent_x, 'ep', split_axis=0, concat_axis=0, tiled=True)  21.6 us
    all_to_all x1, blocking collectives, per_device(): lax.all_to_all(sent_g, 'ep', split_axis=0, concat_axis=0, tiled=True)  19.5 us
    all_to_all x1, waiting for transfers between devices, per_device(): lax.all_to_all(combined.astype(jnp.bfloat16), 'ep', split_axis=0, concat_...  14.9 us
  transfers between devices with their start and end apart: 5, of which 4 were waited for; matrix products, arithmetic and copies ran while one was open for 5% of the time, Pallas kernels for 0%

commit v1 on v0

v1 whole, which is shorter than its diff:
```python
import functools

import jax
import jax.numpy as jnp
from jax import lax
from jax.experimental import pallas as pl
from jax.experimental.pallas import tpu as pltpu
from jax.sharding import PartitionSpec as P

MESH = pl.DeviceIdType.MESH
VMEM_LIMIT = 60 * 1024 * 1024


def greet(n_ep, n_dp, ep, dp):
    barrier = pltpu.get_barrier_semaphore()

    def greet_ep(k, _):
        peer = lax.rem(ep + k + 1, n_ep)
        pl.semaphore_signal(barrier, inc=1, device_id=(peer, dp), device_id_type=MESH)
        return 0

    lax.fori_loop(0, n_ep - 1, greet_ep, 0)
    for t in range(1, n_dp):
        pl.semaphore_signal(
            barrier, inc=1, device_id=(ep, lax.rem(dp + t, n_dp)), device_id_type=MESH
        )
    pl.semaphore_wait(barrier, n_ep + n_dp - 2)


def dispatch_kernel(
    n_ep, n_dp, cap, topk,
    x_ref, c_ref, meta_ref,
    out_x, out_g, meta_out,
    xbuf, cbuf, mbuf, sx, sg,
    zsend, zrecv, esend, erecv, local,
):
    ep, dp = lax.axis_index("ep"), lax.axis_index("dp")
    tok = x_ref.shape[0]
    greet(n_ep, n_dp, ep, dp)

    def along(t):
        target = (ep, lax.rem(dp + n_dp - t, n_dp))
        pairs = ((meta_ref, mbuf), (x_ref, xbuf), (c_ref, cbuf))
        return [
            pltpu.make_async_remote_copy(
                src_ref=src,
                dst_ref=dst.at[t - 1],
                send_sem=zsend.at[t - 1, i],
                recv_sem=zrecv.at[t - 1, i],
                device_id=target,
                device_id_type=MESH,
            )
            for i, (src, dst) in enumerate(pairs)
        ]

    def across(t, k):
        slot = lax.rem(ep + k + 1, n_ep)
        group = lax.rem(dp + t, n_dp)
        return [
            pltpu.make_async_remote_copy(
                src_ref=src.at[t, slot],
                dst_ref=dst.at[group, ep],
                send_sem=esend.at[i, t, k],
                recv_sem=erecv.at[i, t, k],
                device_id=(slot, dp),
                device_id_type=MESH,
            )
            for i, (src, dst) in enumerate(((sx, out_x), (sg, out_g)))
        ]

    def keep(t):
        group = lax.rem(dp + t, n_dp)
        return [
            pltpu.make_async_copy(src.at[t, ep], dst.at[group, ep], local.at[i, t])
            for i, (src, dst) in enumerate(((sx, out_x), (sg, out_g)))
        ]

    for t in range(1, n_dp):
        for copy in along(t):
            copy.start()

    def fill(t, slot, x, c, meta):
        row = (lax.broadcasted_iota(jnp.int32, (cap, tok), 0) + slot * cap).astype(jnp.float32)
        hit = jnp.zeros((cap, tok), jnp.float32)
        weight = jnp.zeros((cap, tok), jnp.float32)
        for k in range(topk):
            same = meta[k : k + 1, :] == row
            hit = jnp.where(same, 1.0, hit)
            weight = jnp.where(same, meta[topk + k : topk + k + 1, :], weight)
        select = hit.astype(jnp.bfloat16)
        weight = jnp.sum(weight, axis=1, keepdims=True)
        sx[t, slot] = jnp.dot(select, x[...], preferred_element_type=jnp.float32).astype(
            jnp.bfloat16
        )
        sg[t, slot] = (
            jnp.dot(select, c[...], preferred_element_type=jnp.float32) * weight
        ).astype(jnp.bfloat16)

    for t in range(n_dp):
        if t == 0:
            x, c, meta_at = x_ref, c_ref, meta_ref
        else:
            for copy in along(t):
                copy.wait_recv()
            x, c, meta_at = xbuf.at[t - 1], cbuf.at[t - 1], mbuf.at[t - 1]
        meta = meta_at[...]
        meta_out[t] = meta

        def step(k, _):
            fill(t, lax.rem(ep + k + 1, n_ep), x, c, meta)
            for copy in across(t, k):
                copy.start()
            return 0

        lax.fori_loop(0, n_ep - 1, step, 0)
        fill(t, ep, x, c, meta)
        for copy in keep(t):
            copy.start()

    for t in range(n_dp):
        def finish(k, _):
            for copy in across(t, k):
                copy.wait_recv()
                copy.wait_send()
            return 0

        lax.fori_loop(0, n_ep - 1, finish, 0)
        for copy in keep(t):
            copy.wait()
        if t > 0:
            for copy in along(t):
                copy.wait_send()


def combine_kernel(
    n_ep, n_dp, cap, topk,
    part, pieces, dest, expert,
    token_out, grad_out,
    back, gbuf, cbuf, zout, zin, total,
    gsend, grecv, csend, crecv, bsend, brecv, zsend, zrecv, local,
):
    ep, dp = lax.axis_index("ep"), lax.axis_index("dp")
    tok = token_out.shape[0]
    rows, width = pieces.shape[1], pieces.shape[2]
    greet(n_ep, n_dp, ep, dp)

    def give(k):
        peer = lax.rem(ep + k + 1, n_ep)
        return pltpu.make_async_remote_copy(
            src_ref=pieces.at[peer],
            dst_ref=gbuf.at[ep],
            send_sem=gsend.at[k],
            recv_sem=grecv.at[k],
            device_id=(peer, dp),
            device_id_type=MESH,
        )

    def hand_back(k):
        peer = lax.rem(ep + k + 1, n_ep)
        return pltpu.make_async_remote_copy(
            src_ref=cbuf.at[peer],
            dst_ref=grad_out.at[ep],
            send_sem=csend.at[k],
            recv_sem=crecv.at[k],
            device_id=(peer, dp),
            device_id_type=MESH,
        )

    def home(t, k):
        peer = lax.rem(ep + k + 1, n_ep)
        return pltpu.make_async_remote_copy(
            src_ref=part.at[lax.rem(dp + t, n_dp), peer],
            dst_ref=back.at[t, ep],
            send_sem=bsend.at[t, k],
            recv_sem=brecv.at[t, k],
            device_id=(peer, dp),
            device_id_type=MESH,
        )

    def along(t):
        return pltpu.make_async_remote_copy(
            src_ref=zout.at[t - 1],
            dst_ref=zin.at[t - 1],
            send_sem=zsend.at[t - 1],
            recv_sem=zrecv.at[t - 1],
            device_id=(ep, lax.rem(dp + t, n_dp)),
            device_id_type=MESH,
        )

    def loop(fn):
        def body(k, _):
            fn(k)
            return 0

        lax.fori_loop(0, n_ep - 1, body, 0)

    order = list(range(1, n_dp)) + [0]
    loop(lambda k: give(k).start())
    for t in order:
        loop(lambda k: home(t, k).start())

    loop(lambda k: give(k).wait_recv())
    gbuf[ep] = pieces[ep]

    def merge(s, _):
        def add(r, acc):
            factor = jnp.where(expert[s] == expert[r], 1.0, 0.0)
            return acc + gbuf[r].astype(jnp.float32) * factor

        acc = lax.fori_loop(0, n_ep, add, jnp.zeros((rows, width), jnp.float32))
        cbuf[s] = acc.astype(jnp.bfloat16)
        return 0

    lax.fori_loop(0, n_ep, merge, 0)
    loop(lambda k: hand_back(k).start())
    own = pltpu.make_async_copy(cbuf.at[ep], grad_out.at[ep], local)
    own.start()

    for t in order:
        loop(lambda k: home(t, k).wait_recv())
        back[t, ep] = part[lax.rem(dp + t, n_dp), ep]
        total[...] = jnp.zeros_like(total)

        def gather(s, _):
            column = (lax.broadcasted_iota(jnp.int32, (tok, cap), 1) + s * cap).astype(jnp.float32)
            hit = jnp.zeros((tok, cap), jnp.float32)
            for k in range(topk):
                hit = jnp.where(dest[t, :, k : k + 1] == column, 1.0, hit)
            total[...] += jnp.dot(
                hit.astype(jnp.bfloat16), back[t, s], preferred_element_type=jnp.float32
            )
            return 0

        lax.fori_loop(0, n_ep, gather, 0)
        if t > 0:
            zout[t - 1] = total[...].astype(jnp.bfloat16)
            along(t).start()

    for t in range(1, n_dp):
        along(t).wait_recv()
        total[...] += zin[t - 1].astype(jnp.float32)
    token_out[...] = total[...].astype(token_out.dtype)

    loop(lambda k: give(k).wait_send())
    loop(lambda k: hand_back(k).wait())
    for t in range(n_dp):
        loop(lambda k: home(t, k).wait_send())
    for t in range(1, n_dp):
        along(t).wait_send()
    own.wait()


def per_device(
    tokens, cotangent, slot_choice, gate_values, slot_expert, gate_weight, up_weight, down_weight
):
    n_ep, n_dp = lax.axis_size("ep"), lax.axis_size("dp")
    tok, width = tokens.shape
    topk = slot_choice.shape[1]
    cap = max(2, 5 * tok * topk // (4 * n_ep))
    flat_slot = slot_choice.reshape(-1)
    onehot = (flat_slot[:, None] == jnp.arange(n_ep, dtype=jnp.int32)[None, :]).astype(jnp.int32)
    position = jnp.sum(jnp.cumsum(onehot, axis=0) * onehot, axis=1) - 1
    dest = (flat_slot * cap + position).reshape(tok, topk)
    lines = -(-2 * topk // 8) * 8
    meta = jnp.concatenate(
        [
            dest.T.astype(jnp.float32),
            gate_values.T,
            jnp.zeros((lines - 2 * topk, tok), jnp.float32),
        ],
        axis=0,
    )
    vmem = pl.BlockSpec(memory_space=pltpu.VMEM)
    anywhere = pl.BlockSpec(memory_space=pl.ANY)
    dma = pltpu.SemaphoreType.DMA
    bf16 = jnp.bfloat16
    routed = jax.ShapeDtypeStruct((n_dp, n_ep, cap, width), bf16)
    rows_x, rows_g, meta_all = pl.pallas_call(
        functools.partial(dispatch_kernel, n_ep, n_dp, cap, topk),
        out_shape=(routed, routed, jax.ShapeDtypeStruct((n_dp, lines, tok), jnp.float32)),
        in_specs=[vmem] * 3,
        out_specs=(anywhere, anywhere, vmem),
        scratch_shapes=[
            pltpu.VMEM((n_dp - 1, tok, width), bf16),
            pltpu.VMEM((n_dp - 1, tok, width), bf16),
            pltpu.VMEM((n_dp - 1, lines, tok), jnp.float32),
            pltpu.VMEM((n_dp, n_ep, cap, width), bf16),
            pltpu.VMEM((n_dp, n_ep, cap, width), bf16),
            dma((n_dp - 1, 3)),
            dma((n_dp - 1, 3)),
            dma((2, n_dp, n_ep)),
            dma((2, n_dp, n_ep)),
            dma((2, n_dp)),
        ],
        compiler_params=pltpu.CompilerParams(
            collective_id=0, has_side_effects=True, vmem_limit_bytes=VMEM_LIMIT
        ),
        name="dispatch",
    )(tokens, cotangent, meta)

    rows_x = rows_x.reshape(-1, width)
    rows_g = rows_g.reshape(-1, width)
    w_gate, w_up, w_down = gate_weight[0], up_weight[0], down_weight[0]
    gate = jnp.dot(rows_x, w_gate, preferred_element_type=jnp.float32)
    up = jnp.dot(rows_x, w_up, preferred_element_type=jnp.float32)
    sig = jax.nn.sigmoid(gate)
    act = (gate * sig * up).astype(bf16)
    d_act = lax.dot_general(
        rows_g, w_down, (((1,), (1,)), ((), ())), preferred_element_type=jnp.float32
    )
    d_gate = (d_act * up * sig * (1.0 + gate * (1.0 - sig))).astype(bf16)
    d_up = (d_act * gate * sig).astype(bf16)
    part = lax.dot_general(
        d_gate, w_gate, (((1,), (1,)), ((), ())), preferred_element_type=jnp.float32
    )
    part = part + lax.dot_general(
        d_up, w_up, (((1,), (1,)), ((), ())), preferred_element_type=jnp.float32
    )
    part = part.astype(bf16).reshape(n_dp, n_ep, cap, width)
    slot_grad = lax.dot_general(
        act, rows_g, (((0,), (0,)), ((), ())), preferred_element_type=jnp.float32
    )
    hidden = slot_grad.shape[0]
    piece = hidden // n_ep
    pieces = slot_grad.astype(bf16).reshape(n_ep, piece, width)

    token_grad, down_grad = pl.pallas_call(
        functools.partial(combine_kernel, n_ep, n_dp, cap, topk),
        out_shape=(
            jax.ShapeDtypeStruct((tok, width), bf16),
            jax.ShapeDtypeStruct((n_ep, piece, width), bf16),
        ),
        in_specs=[vmem, vmem, vmem, pl.BlockSpec(memory_space=pltpu.SMEM)],
        out_specs=(vmem, anywhere),
        scratch_shapes=[
            pltpu.VMEM((n_dp, n_ep, cap, width), bf16),
            pltpu.VMEM((n_ep, piece, width), bf16),
            pltpu.VMEM((n_ep, piece, width), bf16),
            pltpu.VMEM((n_dp - 1, tok, width), bf16),
            pltpu.VMEM((n_dp - 1, tok, width), bf16),
            pltpu.VMEM((tok, width), jnp.float32),
            dma((n_ep,)),
            dma((n_ep,)),
            dma((n_ep,)),
            dma((n_ep,)),
            dma((n_dp, n_ep)),
            dma((n_dp, n_ep)),
            dma((n_dp - 1,)),
            dma((n_dp - 1,)),
            dma,
        ],
        compiler_params=pltpu.CompilerParams(
            collective_id=1, has_side_effects=True, vmem_limit_bytes=VMEM_LIMIT
        ),
        name="combine",
    )(part, pieces, jnp.swapaxes(meta_all[:, :topk, :], 1, 2), slot_expert)
    return token_grad, down_grad.reshape(1, hidden, width)


def solution(mesh):
    return jax.shard_map(
        per_device,
        mesh=mesh,
        in_specs=(
            P(("ep", "dp"), None),
            P(("ep", "dp"), None),
            P(("ep", "dp"), None),
            P(("ep", "dp"), None),
            P(),
            P("ep", None, "dp"),
            P("ep", None, "dp"),
            P("ep", "dp", None),
        ),
        out_specs=(P(("ep", "dp"), None), P("ep", "dp", None)),
        check_vma=False,
    )
```

time: 613 us -> 251 us (0.41)
  blocking collectives: 351 us -> 0 us
  Pallas kernels: 0 us -> 221 us
  waiting for transfers between devices: 170 us -> 0 us
  local copies, waits for them, and re-layouts: 22.5 us -> 7.4 us
  between operations: 14.3 us -> 0.78 us
  matrix products: 30.8 us -> 18.3 us
  starting transfers between devices: 12.3 us -> 0 us
  other arithmetic: 11 us -> 2.77 us
    unnamed x1 -> x0, blocking collectives: 310 us -> none
    pallas_call x0 -> x2, Pallas kernels: none -> 221 us  [the longest x1 139 us: per_device(): pl.pallas_call(functools.partial(dispatch_kernel, n_ep, n_dp, cap, topk),...]
    all_gather x2 -> x0, waiting for transfers between devices: 146 us -> none  [the longest x1 80.2 us: per_device(): lax.all_gather(recv_g, 'dp', axis=0, tiled=True)]
    all_to_all x2 -> x0, blocking collectives: 41.1 us -> none  [the longest x1 21.6 us: per_device(): lax.all_to_all(sent_x, 'ep', split_axis=0, concat_axis=0, tiled=True)]
    all_to_all x3 -> x0, waiting for transfers between devices: 24 us -> none  [the longest x1 14.9 us: per_device(): lax.all_to_all(combined.astype(jnp.bfloat16), 'ep', split_axis=0, concat_...]
    all_to_all x3 -> x0, starting transfers between devices: 12.3 us -> none  [the longest x1 4.54 us: per_device(): lax.all_to_all(pieces, 'ep', split_axis=0, concat_axis=0, tiled=True)]
    all_to_all x3 -> x0, local copies, waits for them, and re-layouts: 10 us -> none  [the longest x1 6.7 us: per_device(): lax.all_to_all(pieces, 'ep', split_axis=0, concat_axis=0, tiled=True)]
    all_to_all x2 -> x0, other arithmetic: 9.48 us -> none  [per_device(): lax.all_to_all(combined.astype(jnp.bfloat16), 'ep', split_axis=0, concat_...]
  transfers between devices with their start and end apart: 5 -> 0, of which waited for: 4 -> 0; matrix products, arithmetic and copies ran while one was open for 5% -> 0% of each run, Pallas kernels for 0% -> 0%
where the time goes in v1:
time: 251 us; the launch traced here: 250 us
  Pallas kernels  221 us (88%)
  matrix products  18.3 us (7%)
  local copies, waits for them, and re-layouts  7.4 us (3%)
  other arithmetic  2.77 us (1%)
    pallas_call x1, Pallas kernels, per_device(): pl.pallas_call(functools.partial(dispatch_kernel, n_ep, n_dp, cap, topk),...  139 us
    pallas_call x1, Pallas kernels, per_device(): pl.pallas_call(functools.partial(combine_kernel, n_ep, n_dp, cap, topk),...  81.9 us
    unnamed x15, local copies, waits for them, and re-layouts  5.04 us

profile of v1, /device:TPU:0, one launch (start us, length us, event | category | flops | bytes accessed | tf_op | source)
XLA Modules:
  0.0 250.1 jit_solution(18072699208187691294)
XLA Ops:
  0.6 0.0 copy-start
  0.7 0.1 pad.2.clone
  0.7 0.9 copy.11
  1.6 0.1 eq.29
  1.7 0.1 eq.25
  1.9 0.6 reduce-window.6
  2.5 0.2 slice_reduce_fusion
  2.7 0.1 fusion.13
  2.8 0.1 sub.10
  3.0 0.1 copy.13
  3.0 0.7 convert_bitcast_fusion
  3.7 1.3 maximum_maximum_fusion.meta_ref
  5.1 139.0 %dispatch.1 = (bf16[4,8,40,1792]{3,2,1,0:T(8,128)(2,1)}, bf16[4,8,40,1792]{3,2,1,0:T(8,128)(2,1)}, f32[4,8,128]{2,1,0:T(8,128)}) custom-call(bf16[128,1792]{1,0:T(8,128)(2,1)} %x_ref.1, bf16[128,1792]{1,0:T(8,128)(2,1)} %c_ref.1, f32[8,128]{1,0:T(8,128)} %maximum_maximum_fusion.meta_ref), custom_call_target="tpu_custom_call" | custom-call | tf_op jit(solution)/shard_map/dispatch/pallas_call | solution.py:278
  144.1 0.7 slice.11
  144.8 0.9 copy.14
  145.7 0.0 copy-done
  145.7 4.1 %fusion.3 = f32[1280,320]{0,1:T(8,128)S(1)} fusion(bf16[1280,1792]{1,0:T(8,128)(2,1)} %bitcast.41, bf16[1,1792,320]{1,2,0:T(8,128)(2,1)S(1)} %copy-done), kind=kOutput, calls=%fused_computation.9 | convolution fusion | flops 1468006400 | bytes 7372800 | tf_op jit(solution)/shard_map/dot_general | solution.py:304
  149.8 0.0 copy-done.1
  149.8 0.0 copy-done.2
  149.9 0.0 slice-start.1
  149.9 1.7 fusion.6
  151.6 0.0 slice-done
  151.6 0.0 slice-done.1
  151.6 0.0 copy-start.3
  151.6 2.9 %convolution_convert_fusion = bf16[320,1792]{1,0:T(8,128)(2,1)} fusion(bf16[1280,1792]{1,0:T(8,128)(2,1)S(1)} %bitcast.39, f32[1280,320]{0,1:T(8,128)S(1)} %fusion.6, f32[1280,320]{0,1:T(8,128)S(1)} %fusion.3), kind=kOutput, calls=%fused_computation.2 | convolution fusion | flops 1471037440 | bytes 9011200 | tf_op jit(solution)/shard_map/dot_general | solution.py:320
  154.5 0.0 copy-done.3
  154.5 1.7 fusion.8
  156.2 2.9 %fusion.1 = f32[1280,1792]{1,0:T(8,128)S(1)} fusion(bf16[1,1792,320]{1,2,0:T(8,128)(2,1)S(1)} %copy-done, f32[1280,320]{0,1:T(8,128)S(1)} %fusion.3, f32[1280,320]{0,1:T(8,128)S(1)} %fusion.8, f32[1280,320]{0,1:T(8,128)S(1)} %fusion.6), kind=kOutput, calls=%fused_computation.7 | convolution fusion | flops 1472102400 | bytes 15237120 | tf_op jit(solution)/shard_map/dot_general | solution.py:313
  159.1 4.9 %fusion = bf16[1280,1792]{1,0:T(8,128)(2,1)} fusion(f32[1280,1792]{1,0:T(8,128)S(1)} %fusion.1, bf16[1,1792,320]{1,2,0:T(8,128)(2,1)S(1)} %copy-done.1, f32[1280,320]{0,1:T(8,128)S(1)} %fusion.8, f32[1280,320]{0,1:T(8,128)S(1)} %fusion.3), kind=kOutput, calls=%fused_computation.1 | convolution fusion | flops 1475051520 | bytes 18186240 | tf_op jit(solution)/shard_map/dot_general | solution.py:316
  164.1 81.9 %combine.1 = (bf16[128,1792]{1,0:T(8,128)(2,1)}, bf16[8,40,1792]{2,1,0:T(8,128)(2,1)}) custom-call(bf16[4,8,40,1792]{3,2,1,0:T(8,128)(2,1)} %bitcast.32, bf16[8,40,1792]{2,1,0:T(8,128)(2,1)} %bitcast.34, f32[4,128,2]{2,1,0:T(8,128)} %bitcast.35, s32[8]{0:T(128)} %expert.1), custom_call_target="tpu_custom_call" | custom-call | tf_op jit(solution)/shard_map/combine/pallas_call | solution.py:327
  246.0 1.8 copy.17
  247.8 2.3 copy.18
  (9 shorter events, 0.1 us)
Async XLA Ops:
  0.6 145.1 %copy-start = (bf16[1,1792,320]{1,2,0:T(8,128)(2,1)S(1)}, bf16[1,1792,320]{1,2,0:T(8,128)(2,1)}, u32[]{:S(2)}) copy-start(bf16[1,1792,320]{1,2,0:T(8,128)(2,1)} %param.13) | copy-start | bytes 3440644
  145.7 4.1 %copy-start.1 = (bf16[1,1792,320]{1,2,0:T(8,128)(2,1)S(1)}, bf16[1,1792,320]{1,2,0:T(8,128)(2,1)}, u32[]{:S(2)}) copy-start(bf16[1,1792,320]{1,2,0:T(8,128)(2,1)} %param.14) | copy-start | bytes 3440644
  145.7 4.2 %copy-start.2 = (bf16[4,8,40,1792]{3,2,1,0:T(8,128)(2,1)S(1)}, bf16[4,8,40,1792]{3,2,1,0:T(8,128)(2,1)}, u32[]{:S(2)}) copy-start(bf16[4,8,40,1792]{3,2,1,0:T(8,128)(2,1)} %get-tuple-element.8) | copy-start | bytes 13762564
  145.7 5.9 %slice-start = ((s8[4587520]{0:T(1024)(128)(4,1)}), s8[4194304]{0:T(1024)(128)(4,1)S(1)}, s32[]{:S(2)}) async-start(s8[4587520]{0:T(1024)(128)(4,1)} %bitcast.37), calls=%async_computation | async-start | bytes 8388608
  149.9 1.7 slice-start.1
  151.6 2.9 %copy-start.3 = (bf16[1,320,1792]{2,1,0:T(8,128)(2,1)S(1)}, bf16[1,320,1792]{2,1,0:T(8,128)(2,1)}, u32[]{:S(2)}) copy-start(bf16[1,320,1792]{2,1,0:T(8,128)(2,1)} %param.15) | copy-start | bytes 3440644

commit v2 on v1

--- a/solution.py
+++ b/solution.py
@@ -28,108 +28,190 @@
 
 
 def dispatch_kernel(
-    n_ep, n_dp, cap, topk,
+    n_ep, n_dp, cap, topk, early, batch,
     x_ref, c_ref, meta_ref,
     out_x, out_g, meta_out,
-    xbuf, cbuf, mbuf, sx, sg,
-    zsend, zrecv, esend, erecv, local,
+    xbuf, cbuf, mbuf, sx_own, sg_own, sx, sg,
+    zsend, zrecv, csend, crecv, esend, erecv, local,
 ):
     ep, dp = lax.axis_index("ep"), lax.axis_index("dp")
-    tok = x_ref.shape[0]
+    tok, width = x_ref.shape
+    late = width - early
+    first, rest = pl.ds(0, early), pl.ds(early, late)
+    outs = (out_x, out_g)
     greet(n_ep, n_dp, ep, dp)
 
-    def along(t):
-        target = (ep, lax.rem(dp + n_dp - t, n_dp))
-        pairs = ((meta_ref, mbuf), (x_ref, xbuf), (c_ref, cbuf))
+    near = [
+        sorted(range(n_dp), key=lambda j: (abs(j - z), -j if 2 * z < n_dp else j))
+        for z in range(n_dp)
+    ]
+
+    def group_of(t):
+        return sum(jnp.where(dp == z, near[z][t], 0) for z in range(n_dp))
+
+    groups = [dp] + [group_of(t) for t in range(1, n_dp)]
+
+    def raw(t, way):
+        g = groups[t]
+        if t == 0:
+            srcs = (meta_ref, x_ref.at[:, rest], c_ref.at[:, rest])
+        else:
+            srcs = (mbuf.at[g], xbuf.at[g], cbuf.at[g])
         return [
             pltpu.make_async_remote_copy(
                 src_ref=src,
-                dst_ref=dst.at[t - 1],
-                send_sem=zsend.at[t - 1, i],
-                recv_sem=zrecv.at[t - 1, i],
-                device_id=target,
+                dst_ref=dst.at[g],
+                send_sem=zsend.at[g, i, way],
+                recv_sem=zrecv.at[g, i],
+                device_id=(ep, lax.rem(dp + n_dp + 1 - 2 * way, n_dp)),
                 device_id_type=MESH,
             )
-            for i, (src, dst) in enumerate(pairs)
+            for i, (src, dst) in enumerate(zip(srcs, (mbuf, xbuf, cbuf)))
         ]
 
-    def across(t, k):
-        slot = lax.rem(ep + k + 1, n_ep)
-        group = lax.rem(dp + t, n_dp)
+    def columns(t, way):
+        g = groups[t]
         return [
             pltpu.make_async_remote_copy(
-                src_ref=src.at[t, slot],
-                dst_ref=dst.at[group, ep],
-                send_sem=esend.at[i, t, k],
-                recv_sem=erecv.at[i, t, k],
+                src_ref=out.at[g, :, :, first],
+                dst_ref=out.at[g, :, :, first],
+                send_sem=csend.at[g, i, way],
+                recv_sem=crecv.at[g, i],
+                device_id=(ep, lax.rem(dp + n_dp + 1 - 2 * way, n_dp)),
+                device_id_type=MESH,
+            )
+            for i, out in enumerate(outs)
+        ]
+
+    def pass_on(make, t, act):
+        g = groups[t]
+
+        @pl.when((g <= dp) & (dp < n_dp - 1))
+        def _():
+            for copy in make(t, 0):
+                act(copy)
+
+        @pl.when((g >= dp) & (dp > 0))
+        def _():
+            for copy in make(t, 1):
+                act(copy)
+
+    def start(copy):
+        copy.start()
+
+    def wait_send(copy):
+        copy.wait_send()
+
+    def ends(t, out, at):
+        g = groups[t]
+        return out.at[g, at] if t == 0 else out.at[g, at, :, rest]
+
+    def made(t):
+        return (sx_own, sg_own) if t == 0 else (sx.at[t - 1], sg.at[t - 1])
+
+    def across(t, slot, source):
+        return [
+            pltpu.make_async_remote_copy(
+                src_ref=src.at[slot],
+                dst_ref=ends(t, out, source),
+                send_sem=esend.at[i, t, slot],
+                recv_sem=erecv.at[i, t, source],
                 device_id=(slot, dp),
                 device_id_type=MESH,
             )
-            for i, (src, dst) in enumerate(((sx, out_x), (sg, out_g)))
+            for i, (src, out) in enumerate(zip(made(t), outs))
         ]
 
     def keep(t):
-        group = lax.rem(dp + t, n_dp)
         return [
-            pltpu.make_async_copy(src.at[t, ep], dst.at[group, ep], local.at[i, t])
-            for i, (src, dst) in enumerate(((sx, out_x), (sg, out_g)))
+            pltpu.make_async_copy(src.at[ep], ends(t, out, ep), local.at[i, t])
+            for i, (src, out) in enumerate(zip(made(t), outs))
         ]
 
-    for t in range(1, n_dp):
-        for copy in along(t):
-            copy.start()
-
-    def fill(t, slot, x, c, meta):
-        row = (lax.broadcasted_iota(jnp.int32, (cap, tok), 0) + slot * cap).astype(jnp.float32)
-        hit = jnp.zeros((cap, tok), jnp.float32)
-        weight = jnp.zeros((cap, tok), jnp.float32)
+    def others(fn):
+        def body(k, _):
+            fn(lax.rem(ep + k + 1, n_ep))
+            return 0
+
+        lax.fori_loop(0, n_ep - 1, body, 0)
+
+    def arrived(t):
+        def body(peer):
+            for copy in across(t, peer, peer):
+                copy.wait_recv()
+
+        others(body)
+        for copy in keep(t):
+            copy.wait()
+
+    def fill(t, base, x, c, meta):
+        shape = (batch * cap, tok)
+        row = (lax.broadcasted_iota(jnp.int32, shape, 0) + base * cap).astype(jnp.float32)
+        hit = jnp.zeros(shape, jnp.float32)
+        weight = jnp.zeros(shape, jnp.float32)
         for k in range(topk):
             same = meta[k : k + 1, :] == row
             hit = jnp.where(same, 1.0, hit)
             weight = jnp.where(same, meta[topk + k : topk + k + 1, :], weight)
         select = hit.astype(jnp.bfloat16)
         weight = jnp.sum(weight, axis=1, keepdims=True)
-        sx[t, slot] = jnp.dot(select, x[...], preferred_element_type=jnp.float32).astype(
-            jnp.bfloat16
-        )
-        sg[t, slot] = (
-            jnp.dot(select, c[...], preferred_element_type=jnp.float32) * weight
-        ).astype(jnp.bfloat16)
-
+        to_x, to_g = made(t)
+        rows = jnp.dot(select, x[...], preferred_element_type=jnp.float32)
+        for i in range(batch):
+            to_x[base + i] = rows[i * cap : (i + 1) * cap].astype(jnp.bfloat16)
+        rows = jnp.dot(select, c[...], preferred_element_type=jnp.float32) * weight
+        for i in range(batch):
+            to_g[base + i] = rows[i * cap : (i + 1) * cap].astype(jnp.bfloat16)
+
+    pass_on(raw, 0, start)
     for t in range(n_dp):
         if t == 0:
             x, c, meta_at = x_ref, c_ref, meta_ref
         else:
-            for copy in along(t):
+            for copy in raw(t, 0):
                 copy.wait_recv()
-            x, c, meta_at = xbuf.at[t - 1], cbuf.at[t - 1], mbuf.at[t - 1]
+            pass_on(raw, t, start)
+            g = groups[t]
+            x, c, meta_at = xbuf.at[g], cbuf.at[g], mbuf.at[g]
         meta = meta_at[...]
-        meta_out[t] = meta
+        meta_out[groups[t]] = meta
 
         def step(k, _):
-            fill(t, lax.rem(ep + k + 1, n_ep), x, c, meta)
-            for copy in across(t, k):
-                copy.start()
+            base = lax.rem((ep // batch + k + 1) * batch, n_ep)
+            fill(t, base, x, c, meta)
+            for i in range(batch):
+                slot = base + lax.rem(ep + i, batch)
+
+                @pl.when(slot != ep)
+                def _():
+                    for copy in across(t, slot, ep):
+                        copy.start()
+
             return 0
 
-        lax.fori_loop(0, n_ep - 1, step, 0)
-        fill(t, ep, x, c, meta)
+        lax.fori_loop(0, n_ep // batch, step, 0)
         for copy in keep(t):
             copy.start()
+        if t == min(2, n_dp - 1):
+            arrived(0)
+            pass_on(columns, 0, start)
+
+    for t in range(1, n_dp):
+        for copy in columns(t, 0):
+            copy.wait_recv()
+        pass_on(columns, t, start)
+    for t in range(1, n_dp):
+        arrived(t)
 
     for t in range(n_dp):
-        def finish(k, _):
-            for copy in across(t, k):
-                copy.wait_recv()
+        pass_on(raw, t, wait_send)
+        pass_on(columns, t, wait_send)
+
+        def sent(peer):
+            for copy in across(t, peer, ep):
                 copy.wait_send()
-            return 0
-
-        lax.fori_loop(0, n_ep - 1, finish, 0)
-        for copy in keep(t):
-            copy.wait()
-        if t > 0:
-            for copy in along(t):
-                copy.wait_send()
+
+        others(sent)
 
 
 def combine_kernel(
@@ -225,7 +307,7 @@
             column = (lax.broadcasted_iota(jnp.int32, (tok, cap), 1) + s * cap).astype(jnp.float32)
             hit = jnp.zeros((tok, cap), jnp.float32)
             for k in range(topk):
-                hit = jnp.where(dest[t, :, k : k + 1] == column, 1.0, hit)
+                hit = jnp.where(dest[lax.rem(dp + t, n_dp), :, k : k + 1] == column, 1.0, hit)
             total[...] += jnp.dot(
                 hit.astype(jnp.bfloat16), back[t, s], preferred_element_type=jnp.float32
             )
@@ -274,20 +356,26 @@
     anywhere = pl.BlockSpec(memory_space=pl.ANY)
     dma = pltpu.SemaphoreType.DMA
     bf16 = jnp.bfloat16
+    early = 3 * width // (14 * 128) * 128
+    batch = 4 if cap % 8 == 0 and n_ep % 4 == 0 else 1
     routed = jax.ShapeDtypeStruct((n_dp, n_ep, cap, width), bf16)
     rows_x, rows_g, meta_all = pl.pallas_call(
-        functools.partial(dispatch_kernel, n_ep, n_dp, cap, topk),
+        functools.partial(dispatch_kernel, n_ep, n_dp, cap, topk, early, batch),
         out_shape=(routed, routed, jax.ShapeDtypeStruct((n_dp, lines, tok), jnp.float32)),
         in_specs=[vmem] * 3,
         out_specs=(anywhere, anywhere, vmem),
         scratch_shapes=[
-            pltpu.VMEM((n_dp - 1, tok, width), bf16),
-            pltpu.VMEM((n_dp - 1, tok, width), bf16),
-            pltpu.VMEM((n_dp - 1, lines, tok), jnp.float32),
-            pltpu.VMEM((n_dp, n_ep, cap, width), bf16),
-            pltpu.VMEM((n_dp, n_ep, cap, width), bf16),
-            dma((n_dp - 1, 3)),
-            dma((n_dp - 1, 3)),
+            pltpu.VMEM((n_dp, tok, width - early), bf16),
+            pltpu.VMEM((n_dp, tok, width - early), bf16),
+            pltpu.VMEM((n_dp, lines, tok), jnp.float32),
+            pltpu.VMEM((n_ep, cap, width), bf16),
+            pltpu.VMEM((n_ep, cap, width), bf16),
+            pltpu.VMEM((n_dp - 1, n_ep, cap, width - early), bf16),
+            pltpu.VMEM((n_dp - 1, n_ep, cap, width - early), bf16),
+            dma((n_dp, 3, 2)),
+            dma((n_dp, 3)),
+            dma((n_dp, 2, 2)),
+            dma((n_dp, 2)),
             dma((2, n_dp, n_ep)),
             dma((2, n_dp, n_ep)),
             dma((2, n_dp)),

time: 251 us -> 206 us (0.82)
  Pallas kernels: 221 us -> 175 us
    pallas_call x1, Pallas kernels: 139 us -> 93.2 us  [per_device(): pl.pallas_call(functools.partial(dispatch_kernel, n_ep, n_dp, cap, topk,...]
where the time goes in v2:
time: 206 us; the launch traced here: 204 us
  Pallas kernels  175 us (85%)
  matrix products  18.3 us (9%)
  local copies, waits for them, and re-layouts  7.4 us (4%)
  other arithmetic  2.77 us (1%)
    pallas_call x1, Pallas kernels, per_device(): pl.pallas_call(functools.partial(dispatch_kernel, n_ep, n_dp, cap, topk,...  93.2 us
    pallas_call x1, Pallas kernels, per_device(): pl.pallas_call(functools.partial(combine_kernel, n_ep, n_dp, cap, topk),...  81.9 us
    unnamed x15, local copies, waits for them, and re-layouts  5.04 us
    dot_general x1, matrix products, per_device(): lax.dot_general(d_up, w_up, (((1,), (1,)), ((), ())), preferred_element_t...  4.93 us
    dot_general x1, matrix products, per_device(): gate = jnp.dot(rows_x, w_gate, preferred_element_type=jnp.float32)  4.13 us

profile of v2, /device:TPU:0, one launch (start us, length us, event | category | flops | bytes accessed | tf_op | source)
XLA Modules:
  0.0 204.2 jit_solution(693424166277765810)
XLA Ops:
  0.6 0.0 copy-start
  0.7 0.1 pad.2.clone
  0.7 0.9 copy.11
  1.6 0.1 eq.29
  1.7 0.1 eq.25
  1.9 0.6 reduce-window.6
  2.5 0.2 slice_reduce_fusion
  2.7 0.1 fusion.13
  2.8 0.1 sub.10
  3.0 0.1 copy.13
  3.0 0.7 convert_bitcast_fusion
  3.7 1.3 maximum_maximum_fusion.meta_ref
  5.1 93.2 %dispatch.1 = (bf16[4,8,40,1792]{3,2,1,0:T(8,128)(2,1)}, bf16[4,8,40,1792]{3,2,1,0:T(8,128)(2,1)}, f32[4,8,128]{2,1,0:T(8,128)}) custom-call(bf16[128,1792]{1,0:T(8,128)(2,1)} %x_ref.1, bf16[128,1792]{1,0:T(8,128)(2,1)} %c_ref.1, f32[8,128]{1,0:T(8,128)} %maximum_maximum_fusion.meta_ref), custom_call_target="tpu_custom_call" | custom-call | tf_op jit(solution)/shard_map/dispatch/pallas_call | solution.py:362
  98.3 0.7 slice.11
  99.0 0.9 copy.14
  99.8 0.0 copy-done
  99.9 4.1 %fusion.3 = f32[1280,320]{0,1:T(8,128)S(1)} fusion(bf16[1280,1792]{1,0:T(8,128)(2,1)} %bitcast.41, bf16[1,1792,320]{1,2,0:T(8,128)(2,1)S(1)} %copy-done), kind=kOutput, calls=%fused_computation.9 | convolution fusion | flops 1468006400 | bytes 7372800 | tf_op jit(solution)/shard_map/dot_general | solution.py:392
  104.0 0.0 copy-done.1
  104.0 0.0 copy-done.2
  104.0 0.0 slice-start.1
  104.0 1.7 fusion.6
  105.7 0.0 slice-done
  105.7 0.0 slice-done.1
  105.7 0.0 copy-start.3
  105.7 2.9 %convolution_convert_fusion = bf16[320,1792]{1,0:T(8,128)(2,1)} fusion(bf16[1280,1792]{1,0:T(8,128)(2,1)S(1)} %bitcast.39, f32[1280,320]{0,1:T(8,128)S(1)} %fusion.6, f32[1280,320]{0,1:T(8,128)S(1)} %fusion.3), kind=kOutput, calls=%fused_computation.2 | convolution fusion | flops 1471037440 | bytes 9011200 | tf_op jit(solution)/shard_map/dot_general | solution.py:408
  108.7 0.0 copy-done.3
  108.7 1.7 fusion.8
  110.3 2.9 %fusion.1 = f32[1280,1792]{1,0:T(8,128)S(1)} fusion(bf16[1,1792,320]{1,2,0:T(8,128)(2,1)S(1)} %copy-done, f32[1280,320]{0,1:T(8,128)S(1)} %fusion.3, f32[1280,320]{0,1:T(8,128)S(1)} %fusion.8, f32[1280,320]{0,1:T(8,128)S(1)} %fusion.6), kind=kOutput, calls=%fused_computation.7 | convolution fusion | flops 1472102400 | bytes 15237120 | tf_op jit(solution)/shard_map/dot_general | solution.py:401
  113.3 4.9 %fusion = bf16[1280,1792]{1,0:T(8,128)(2,1)} fusion(f32[1280,1792]{1,0:T(8,128)S(1)} %fusion.1, bf16[1,1792,320]{1,2,0:T(8,128)(2,1)S(1)} %copy-done.1, f32[1280,320]{0,1:T(8,128)S(1)} %fusion.8, f32[1280,320]{0,1:T(8,128)S(1)} %fusion.3), kind=kOutput, calls=%fused_computation.1 | convolution fusion | flops 1475051520 | bytes 18186240 | tf_op jit(solution)/shard_map/dot_general | solution.py:404
  118.2 81.9 %combine.1 = (bf16[128,1792]{1,0:T(8,128)(2,1)}, bf16[8,40,1792]{2,1,0:T(8,128)(2,1)}) custom-call(bf16[4,8,40,1792]{3,2,1,0:T(8,128)(2,1)} %bitcast.32, bf16[8,40,1792]{2,1,0:T(8,128)(2,1)} %bitcast.34, f32[4,128,2]{2,1,0:T(8,128)} %bitcast.35, s32[8]{0:T(128)} %expert.1), custom_call_target="tpu_custom_call" | custom-call | tf_op jit(solution)/shard_map/combine/pallas_call | solution.py:415
  200.1 1.8 copy.17
  201.9 2.3 %copy.18 = bf16[1,320,1792]{2,1,0:T(8,128)(2,1)} copy(bf16[1,320,1792]{2,1,0:T(8,128)(2,1)} %bitcast.33) | data formatting | bytes 2293760
  (9 shorter events, 0.1 us)
Async XLA Ops:
  0.6 99.2 %copy-start = (bf16[1,1792,320]{1,2,0:T(8,128)(2,1)S(1)}, bf16[1,1792,320]{1,2,0:T(8,128)(2,1)}, u32[]{:S(2)}) copy-start(bf16[1,1792,320]{1,2,0:T(8,128)(2,1)} %param.13) | copy-start | bytes 3440644
  99.8 4.1 %copy-start.1 = (bf16[1,1792,320]{1,2,0:T(8,128)(2,1)S(1)}, bf16[1,1792,320]{1,2,0:T(8,128)(2,1)}, u32[]{:S(2)}) copy-start(bf16[1,1792,320]{1,2,0:T(8,128)(2,1)} %param.14) | copy-start | bytes 3440644
  99.8 4.2 %copy-start.2 = (bf16[4,8,40,1792]{3,2,1,0:T(8,128)(2,1)S(1)}, bf16[4,8,40,1792]{3,2,1,0:T(8,128)(2,1)}, u32[]{:S(2)}) copy-start(bf16[4,8,40,1792]{3,2,1,0:T(8,128)(2,1)} %get-tuple-element.8) | copy-start | bytes 13762564
  99.8 5.9 %slice-start = ((s8[4587520]{0:T(1024)(128)(4,1)}), s8[4194304]{0:T(1024)(128)(4,1)S(1)}, s32[]{:S(2)}) async-start(s8[4587520]{0:T(1024)(128)(4,1)} %bitcast.37), calls=%async_computation | async-start | bytes 8388608
  104.0 1.7 slice-start.1
  105.7 2.9 %copy-start.3 = (bf16[1,320,1792]{2,1,0:T(8,128)(2,1)S(1)}, bf16[1,320,1792]{2,1,0:T(8,128)(2,1)}, u32[]{:S(2)}) copy-start(bf16[1,320,1792]{2,1,0:T(8,128)(2,1)} %param.15) | copy-start | bytes 3440644

commit v3 on v2

--- a/solution.py
+++ b/solution.py
@@ -215,14 +215,15 @@
 
 
 def combine_kernel(
-    n_ep, n_dp, cap, topk,
+    n_ep, n_dp, cap, topk, early,
     part, pieces, dest, expert,
     token_out, grad_out,
-    back, gbuf, cbuf, zout, zin, total,
-    gsend, grecv, csend, crecv, bsend, brecv, zsend, zrecv, local,
+    back, gbuf, cbuf, zout, zin, total, shares, mine,
+    gsend, grecv, csend, crecv, bsend, brecv, zsend, zrecv, hsend, hrecv, msend, mrecv, local,
 ):
     ep, dp = lax.axis_index("ep"), lax.axis_index("dp")
     tok = token_out.shape[0]
+    first, rest = pl.ds(0, early), pl.ds(early, pieces.shape[2] - early)
     rows, width = pieces.shape[1], pieces.shape[2]
     greet(n_ep, n_dp, ep, dp)
 
@@ -251,8 +252,8 @@
     def home(t, k):
         peer = lax.rem(ep + k + 1, n_ep)
         return pltpu.make_async_remote_copy(
-            src_ref=part.at[lax.rem(dp + t, n_dp), peer],
-            dst_ref=back.at[t, ep],
+            src_ref=part.at[lax.rem(dp + t, n_dp), peer, :, rest],
+            dst_ref=back.at[t, ep, :, rest],
             send_sem=bsend.at[t, k],
             recv_sem=brecv.at[t, k],
             device_id=(peer, dp),
@@ -269,6 +270,28 @@
             device_id_type=MESH,
         )
 
+    def share(t):
+        target = lax.rem(dp + t, n_dp)
+        return pltpu.make_async_remote_copy(
+            src_ref=part.at[target, :, :, first],
+            dst_ref=shares.at[t - 1],
+            send_sem=hsend.at[t - 1],
+            recv_sem=hrecv.at[t - 1],
+            device_id=(ep, target),
+            device_id_type=MESH,
+        )
+
+    def bring(k):
+        peer = lax.rem(ep + k + 1, n_ep)
+        return pltpu.make_async_remote_copy(
+            src_ref=mine.at[peer],
+            dst_ref=back.at[0, ep, :, first],
+            send_sem=msend.at[k],
+            recv_sem=mrecv.at[k],
+            device_id=(peer, dp),
+            device_id_type=MESH,
+        )
+
     def loop(fn):
         def body(k, _):
             fn(k)
@@ -278,6 +301,8 @@
 
     order = list(range(1, n_dp)) + [0]
     loop(lambda k: give(k).start())
+    for t in range(1, n_dp):
+        share(t).start()
     for t in order:
         loop(lambda k: home(t, k).start())
 
@@ -298,9 +323,26 @@
     own = pltpu.make_async_copy(cbuf.at[ep], grad_out.at[ep], local)
     own.start()
 
+    for t in range(1, n_dp):
+        share(t).wait_recv()
+
+    def sum_share(e, _):
+        acc = part[dp, e, :, first].astype(jnp.float32)
+        for t in range(1, n_dp):
+            acc = acc + shares[t - 1, e].astype(jnp.float32)
+        mine[e] = acc.astype(jnp.bfloat16)
+        return 0
+
+    lax.fori_loop(0, n_ep, sum_share, 0)
+    loop(lambda k: bring(k).start())
+    back[0, ep, :, first] = mine[ep]
+
     for t in order:
         loop(lambda k: home(t, k).wait_recv())
-        back[t, ep] = part[lax.rem(dp + t, n_dp), ep]
+        back[t, ep, :, rest] = part[lax.rem(dp + t, n_dp), ep, :, rest]
+        if t == 0:
+            loop(lambda k: bring(k).wait_recv())
+        used = pl.ds(0, pieces.shape[2]) if t == 0 else rest
         total[...] = jnp.zeros_like(total)
 
         def gather(s, _):
@@ -308,19 +350,19 @@
             hit = jnp.zeros((tok, cap), jnp.float32)
             for k in range(topk):
                 hit = jnp.where(dest[lax.rem(dp + t, n_dp), :, k : k + 1] == column, 1.0, hit)
-            total[...] += jnp.dot(
-                hit.astype(jnp.bfloat16), back[t, s], preferred_element_type=jnp.float32
+            total[:, used] += jnp.dot(
+                hit.astype(jnp.bfloat16), back[t, s, :, used], preferred_element_type=jnp.float32
             )
             return 0
 
         lax.fori_loop(0, n_ep, gather, 0)
         if t > 0:
-            zout[t - 1] = total[...].astype(jnp.bfloat16)
+            zout[t - 1] = total[:, rest].astype(jnp.bfloat16)
             along(t).start()
 
     for t in range(1, n_dp):
         along(t).wait_recv()
-        total[...] += zin[t - 1].astype(jnp.float32)
+        total[:, rest] += zin[t - 1].astype(jnp.float32)
     token_out[...] = total[...].astype(token_out.dtype)
 
     loop(lambda k: give(k).wait_send())
@@ -329,6 +371,8 @@
         loop(lambda k: home(t, k).wait_send())
     for t in range(1, n_dp):
         along(t).wait_send()
+        share(t).wait_send()
+    loop(lambda k: bring(k).wait_send())
     own.wait()
 
 
@@ -413,7 +457,7 @@
     pieces = slot_grad.astype(bf16).reshape(n_ep, piece, width)
 
     token_grad, down_grad = pl.pallas_call(
-        functools.partial(combine_kernel, n_ep, n_dp, cap, topk),
+        functools.partial(combine_kernel, n_ep, n_dp, cap, topk, early),
         out_shape=(
             jax.ShapeDtypeStruct((tok, width), bf16),
             jax.ShapeDtypeStruct((n_ep, piece, width), bf16),
@@ -424,9 +468,11 @@
             pltpu.VMEM((n_dp, n_ep, cap, width), bf16),
             pltpu.VMEM((n_ep, piece, width), bf16),
             pltpu.VMEM((n_ep, piece, width), bf16),
-            pltpu.VMEM((n_dp - 1, tok, width), bf16),
-            pltpu.VMEM((n_dp - 1, tok, width), bf16),
+            pltpu.VMEM((n_dp - 1, tok, width - early), bf16),
+            pltpu.VMEM((n_dp - 1, tok, width - early), bf16),
             pltpu.VMEM((tok, width), jnp.float32),
+            pltpu.VMEM((n_dp - 1, n_ep, cap, early), bf16),
+            pltpu.VMEM((n_ep, cap, early), bf16),
             dma((n_ep,)),
             dma((n_ep,)),
             dma((n_ep,)),
@@ -435,6 +481,10 @@
             dma((n_dp, n_ep)),
             dma((n_dp - 1,)),
             dma((n_dp - 1,)),
+            dma((n_dp - 1,)),
+            dma((n_dp - 1,)),
+            dma((n_ep,)),
+            dma((n_ep,)),
             dma,
         ],
         compiler_params=pltpu.CompilerParams(

time: 206 us -> 202 us (0.981)
  Pallas kernels: 175 us -> 172 us
    pallas_call x1, Pallas kernels: 81.9 us -> 78.8 us  [per_device(): pl.pallas_call(functools.partial(combine_kernel, n_ep, n_dp, cap, topk, e...]
where the time goes in v3:
time: 202 us; the launch traced here: 201 us
  Pallas kernels  172 us (85%)
  matrix products  18.3 us (9%)
  local copies, waits for them, and re-layouts  7.4 us (4%)
  other arithmetic  2.77 us (1%)
    pallas_call x1, Pallas kernels, per_device(): pl.pallas_call(functools.partial(dispatch_kernel, n_ep, n_dp, cap, topk,...  93.2 us
    pallas_call x1, Pallas kernels, per_device(): pl.pallas_call(functools.partial(combine_kernel, n_ep, n_dp, cap, topk, e...  78.8 us
    unnamed x15, local copies, waits for them, and re-layouts  5.04 us
    dot_general x1, matrix products, per_device(): lax.dot_general(d_up, w_up, (((1,), (1,)), ((), ())), preferred_element_t...  4.93 us
    dot_general x1, matrix products, per_device(): gate = jnp.dot(rows_x, w_gate, preferred_element_type=jnp.float32)  4.13 us

profile of v3, /device:TPU:0, one launch (start us, length us, event | category | flops | bytes accessed | tf_op | source)
XLA Modules:
  0.0 201.2 jit_solution(18307624090570043439)
XLA Ops:
  0.6 0.0 copy-start
  0.7 0.1 pad.2.clone
  0.7 0.9 copy.11
  1.6 0.1 eq.29
  1.7 0.1 eq.25
  1.9 0.6 reduce-window.6
  2.5 0.2 slice_reduce_fusion
  2.7 0.1 fusion.13
  2.8 0.1 sub.10
  3.0 0.1 copy.13
  3.0 0.7 convert_bitcast_fusion
  3.7 1.3 maximum_maximum_fusion.meta_ref
  5.1 93.2 %dispatch.1 = (bf16[4,8,40,1792]{3,2,1,0:T(8,128)(2,1)}, bf16[4,8,40,1792]{3,2,1,0:T(8,128)(2,1)}, f32[4,8,128]{2,1,0:T(8,128)}) custom-call(bf16[128,1792]{1,0:T(8,128)(2,1)} %x_ref.1, bf16[128,1792]{1,0:T(8,128)(2,1)} %c_ref.1, f32[8,128]{1,0:T(8,128)} %maximum_maximum_fusion.meta_ref), custom_call_target="tpu_custom_call" | custom-call | tf_op jit(solution)/shard_map/dispatch/pallas_call | solution.py:406
  98.3 0.7 slice.11
  99.0 0.9 copy.14
  99.8 0.0 copy-done
  99.9 4.1 %fusion.3 = f32[1280,320]{0,1:T(8,128)S(1)} fusion(bf16[1280,1792]{1,0:T(8,128)(2,1)} %bitcast.41, bf16[1,1792,320]{1,2,0:T(8,128)(2,1)S(1)} %copy-done), kind=kOutput, calls=%fused_computation.9 | convolution fusion | flops 1468006400 | bytes 7372800 | tf_op jit(solution)/shard_map/dot_general | solution.py:436
  104.0 0.0 copy-done.1
  104.0 0.0 copy-done.2
  104.0 0.0 slice-start.1
  104.0 1.7 fusion.6
  105.7 0.0 slice-done
  105.7 0.0 slice-done.1
  105.7 0.0 copy-start.3
  105.7 2.9 %convolution_convert_fusion = bf16[320,1792]{1,0:T(8,128)(2,1)} fusion(bf16[1280,1792]{1,0:T(8,128)(2,1)S(1)} %bitcast.39, f32[1280,320]{0,1:T(8,128)S(1)} %fusion.6, f32[1280,320]{0,1:T(8,128)S(1)} %fusion.3), kind=kOutput, calls=%fused_computation.2 | convolution fusion | flops 1471037440 | bytes 9011200 | tf_op jit(solution)/shard_map/dot_general | solution.py:452
  108.7 0.0 copy-done.3
  108.7 1.7 fusion.8
  110.3 2.9 %fusion.1 = f32[1280,1792]{1,0:T(8,128)S(1)} fusion(bf16[1,1792,320]{1,2,0:T(8,128)(2,1)S(1)} %copy-done, f32[1280,320]{0,1:T(8,128)S(1)} %fusion.3, f32[1280,320]{0,1:T(8,128)S(1)} %fusion.8, f32[1280,320]{0,1:T(8,128)S(1)} %fusion.6), kind=kOutput, calls=%fused_computation.7 | convolution fusion | flops 1472102400 | bytes 15237120 | tf_op jit(solution)/shard_map/dot_general | solution.py:445
  113.3 4.9 %fusion = bf16[1280,1792]{1,0:T(8,128)(2,1)} fusion(f32[1280,1792]{1,0:T(8,128)S(1)} %fusion.1, bf16[1,1792,320]{1,2,0:T(8,128)(2,1)S(1)} %copy-done.1, f32[1280,320]{0,1:T(8,128)S(1)} %fusion.8, f32[1280,320]{0,1:T(8,128)S(1)} %fusion.3), kind=kOutput, calls=%fused_computation.1 | convolution fusion | flops 1475051520 | bytes 18186240 | tf_op jit(solution)/shard_map/dot_general | solution.py:448
  118.2 78.8 %combine.1 = (bf16[128,1792]{1,0:T(8,128)(2,1)}, bf16[8,40,1792]{2,1,0:T(8,128)(2,1)}) custom-call(bf16[4,8,40,1792]{3,2,1,0:T(8,128)(2,1)} %bitcast.32, bf16[8,40,1792]{2,1,0:T(8,128)(2,1)} %bitcast.34, f32[4,128,2]{2,1,0:T(8,128)} %bitcast.35, s32[8]{0:T(128)} %expert.1), custom_call_target="tpu_custom_call" | custom-call | tf_op jit(solution)/shard_map/combine/pallas_call | solution.py:459
  197.0 1.8 copy.17
  198.8 2.3 %copy.18 = bf16[1,320,1792]{2,1,0:T(8,128)(2,1)} copy(bf16[1,320,1792]{2,1,0:T(8,128)(2,1)} %bitcast.33) | data formatting | bytes 2293760
  (9 shorter events, 0.1 us)
Async XLA Ops:
  0.6 99.2 %copy-start = (bf16[1,1792,320]{1,2,0:T(8,128)(2,1)S(1)}, bf16[1,1792,320]{1,2,0:T(8,128)(2,1)}, u32[]{:S(2)}) copy-start(bf16[1,1792,320]{1,2,0:T(8,128)(2,1)} %param.13) | copy-start | bytes 3440644
  99.8 4.1 %copy-start.1 = (bf16[1,1792,320]{1,2,0:T(8,128)(2,1)S(1)}, bf16[1,1792,320]{1,2,0:T(8,128)(2,1)}, u32[]{:S(2)}) copy-start(bf16[1,1792,320]{1,2,0:T(8,128)(2,1)} %param.14) | copy-start | bytes 3440644
  99.8 4.2 %copy-start.2 = (bf16[4,8,40,1792]{3,2,1,0:T(8,128)(2,1)S(1)}, bf16[4,8,40,1792]{3,2,1,0:T(8,128)(2,1)}, u32[]{:S(2)}) copy-start(bf16[4,8,40,1792]{3,2,1,0:T(8,128)(2,1)} %get-tuple-element.8) | copy-start | bytes 13762564
  99.8 5.9 %slice-start = ((s8[4587520]{0:T(1024)(128)(4,1)}), s8[4194304]{0:T(1024)(128)(4,1)S(1)}, s32[]{:S(2)}) async-start(s8[4587520]{0:T(1024)(128)(4,1)} %bitcast.37), calls=%async_computation | async-start | bytes 8388608
  104.0 1.7 slice-start.1
  105.7 2.9 %copy-start.3 = (bf16[1,320,1792]{2,1,0:T(8,128)(2,1)S(1)}, bf16[1,320,1792]{2,1,0:T(8,128)(2,1)}, u32[]{:S(2)}) copy-start(bf16[1,320,1792]{2,1,0:T(8,128)(2,1)} %param.15) | copy-start | bytes 3440644
